TPU v7x, 32 devices: a whole 2x2x4 slice. The times are simulated.
32 devices in a mesh: seq: 4 (over y, core), fsdp: 8 (over z, x).
Axes of the slice: x: 2, y: 2, z: 4, core: 2. Of those that a mesh axis runs over, the one named last changes fastest.
Arguments:
- tokens: bfloat16 [8, 1024, 2048], P('fsdp', 'seq'), may hold values from -6 to 6
- teacher: bfloat16 [8, 1024, 2048], P('fsdp', 'seq'), may hold values from -6 to 6
- segments: int32 [8, 1024], P('fsdp'), may hold values from 0 to 3, never falling along the last dimension, each value on 1 to 512 neighbouring positions
- valid: int32 [8, 1024], P('fsdp', 'seq'), may hold values from 0 to 1, as said below
- ln1_gain: bfloat16 [2048], P('fsdp'), may hold values from 0.099609375 to 1.8984375
- ln1_bias: bfloat16 [2048], P('fsdp'), may hold values from -1.75 to 1.75
- w_qkv: bfloat16 [2048, 6144], P('fsdp'), may hold values from -0.125 to 0.125
- b_qkv: bfloat16 [6144], P('fsdp'), may hold values from -1.75 to 1.75
- w_out: bfloat16 [2048, 2048], P('fsdp'), may hold values from -0.5 to 0.5
- ln2_gain: bfloat16 [2048], P('fsdp'), may hold values from 0.099609375 to 1.8984375
- ln2_bias: bfloat16 [2048], P('fsdp'), may hold values from -1.75 to 1.75
- w_gate_up: bfloat16 [5632, 2, 2048], P('fsdp'), may hold values from -0.125 to 0.125
- w_down: bfloat16 [5632, 2048], P('fsdp'), may hold values from -0.15625 to 0.15625
Outputs:
- layer_out: bfloat16 [8, 1024, 2048], P('fsdp', 'seq')
- loss: float32 [], replicated
- grad_tokens: bfloat16 [8, 1024, 2048], P('fsdp', 'seq')
- grad_ln1_gain: float32 [2048], P('fsdp')
- grad_ln1_bias: float32 [2048], P('fsdp')
- grad_w_qkv: float32 [2048, 6144], P('fsdp')
- grad_b_qkv: float32 [6144], P('fsdp')
- grad_w_out: float32 [2048, 2048], P('fsdp')
- grad_ln2_gain: float32 [2048], P('fsdp')
- grad_ln2_bias: float32 [2048], P('fsdp')
- grad_w_gate_up: float32 [5632, 2, 2048], P('fsdp')
- grad_w_down: float32 [5632, 2048], P('fsdp')
Inputs may be any that keep to these rules, and one draw needn't show every extreme that they name: `segments`: segment numbers start at 0 in each sequence and never fall; each document has 1 to 512 tokens and one document of each sequence has exactly that many. `valid`: the first token of every sequence counts.
All inputs are finite; a program needn't handle non-finite values.
Results may differ from a plain program's by a relative error of at most 0.01.
Values may be sent and summed in bfloat16 or wider, within the bound.
No kernel may reach another device: no remote copies, remote signals or barrier semaphores. Data moves between devices by JAX's collectives and lax.ppermute only.
A program may use at most 704 MiB of HBM per device.

v0:
```python
import jax
import jax.numpy as jnp
from jax import lax
from jax.sharding import PartitionSpec as P

H = 32
HD = 64
ROT = 16
EPSILON = 1e-05
MASKED_VALUE = -1e30


def norm_parts(values):
    mean_value = jnp.mean(values, axis=-1, keepdims=True)
    centered = values - mean_value
    variance = jnp.mean(centered * centered, axis=-1, keepdims=True)
    inv_std = lax.rsqrt(variance + EPSILON)
    return (centered * inv_std, inv_std)


def norm_back(grad_out, normed, inv_std, gain_vec):
    scaled = grad_out * gain_vec
    mean_scaled = jnp.mean(scaled, axis=-1, keepdims=True)
    mean_cross = jnp.mean(scaled * normed, axis=-1, keepdims=True)
    return inv_std * (scaled - mean_scaled - normed * mean_cross)


def doc_positions(segment):
    places = jnp.arange(segment.shape[0], dtype=jnp.int32)
    change = jnp.concatenate([jnp.ones((1,), dtype=bool), segment[1:] != segment[:-1]])
    starts = lax.cummax(jnp.where(change, places, 0), axis=0)
    return places - starts


def rotate(values, positions, turn_sign):
    half_rot = ROT // 2
    inverse = 10000.0 ** (-(jnp.arange(half_rot, dtype=jnp.float32) * 2.0) / ROT)
    angles = positions.astype(jnp.float32)[:, None] * inverse[None, :]
    cosine = jnp.cos(angles)[:, None, :]
    sine_part = turn_sign * jnp.sin(angles)[:, None, :]
    front_half = values[..., :half_rot]
    back_half = values[..., half_rot:ROT]
    return jnp.concatenate(
        [
            front_half * cosine - back_half * sine_part,
            back_half * cosine + front_half * sine_part,
            values[..., ROT:],
        ],
        axis=-1,
    )


def gate_backward(gate_up, hidden_grad):
    gate_part = gate_up[:, 0]
    up_part = gate_up[:, 1]
    gate_sig = jax.nn.sigmoid(gate_part)
    up_grad = hidden_grad * (gate_part * gate_sig)
    silu_grad = hidden_grad * up_part
    gate_grad = silu_grad * gate_sig + silu_grad * gate_part * gate_sig * (1.0 - gate_sig)
    return jnp.stack([gate_grad, up_grad], axis=1).astype(jnp.bfloat16)


def block_scores(query_block, key_rows, block_seg, segment, first_row, score_scale):
    block_size = query_block.shape[0]
    places = jnp.arange(segment.shape[0], dtype=jnp.int32)
    block_places = first_row + jnp.arange(block_size, dtype=jnp.int32)
    allowed = (block_seg[:, None] == segment[None, :]) & (block_places[:, None] >= places[None, :])
    scores = (
        jnp.einsum("bhd,lhd->hbl", query_block, key_rows, preferred_element_type=jnp.float32)
        * score_scale
    )
    return jnp.where(allowed[None], scores, MASKED_VALUE)


def attention_forward(query_rows, key_rows, value_rows, segment, block_size, score_scale):
    length_total = key_rows.shape[0]

    def one_block(unused, first_row):
        query_block = lax.dynamic_slice_in_dim(query_rows, first_row, block_size, 0)
        block_seg = lax.dynamic_slice_in_dim(segment, first_row, block_size, 0)
        scores = block_scores(query_block, key_rows, block_seg, segment, first_row, score_scale)
        row_max = jnp.max(scores, axis=-1, keepdims=True)
        exp_scores = jnp.exp(scores - row_max)
        row_sum = jnp.sum(exp_scores, axis=-1, keepdims=True)
        probs = (exp_scores / row_sum).astype(jnp.bfloat16)
        block_out = jnp.einsum(
            "hbl,lhd->bhd", probs, value_rows, preferred_element_type=jnp.float32
        )
        return (unused, (block_out.astype(jnp.bfloat16), (row_max + jnp.log(row_sum))[..., 0]))

    firsts = jnp.arange(length_total // block_size, dtype=jnp.int32) * block_size
    unused, (block_outs, log_totals) = lax.scan(one_block, jnp.zeros((), jnp.int32), firsts)
    return (block_outs.reshape(length_total, query_rows.shape[1], query_rows.shape[2]), log_totals)


def attention_backward(
    query_rows, key_rows, value_rows, out_grad, log_totals, segment, block_size, score_scale
):
    length_total = key_rows.shape[0]

    def one_block(grad_carry, block_inputs):
        key_grad, value_grad = grad_carry
        first_row, block_log = block_inputs
        query_block = lax.dynamic_slice_in_dim(query_rows, first_row, block_size, 0)
        grad_block = lax.dynamic_slice_in_dim(out_grad, first_row, block_size, 0)
        block_seg = lax.dynamic_slice_in_dim(segment, first_row, block_size, 0)
        scores = block_scores(query_block, key_rows, block_seg, segment, first_row, score_scale)
        probs = jnp.exp(scores - block_log[..., None])
        prob_low = probs.astype(jnp.bfloat16)
        value_grad = value_grad + jnp.einsum(
            "hbl,bhd->lhd", prob_low, grad_block, preferred_element_type=jnp.float32
        )
        prob_grad = jnp.einsum(
            "bhd,lhd->hbl", grad_block, value_rows, preferred_element_type=jnp.float32
        )
        row_dot = jnp.sum(probs * prob_grad, axis=-1, keepdims=True)
        score_grad = (probs * (prob_grad - row_dot)).astype(jnp.bfloat16)
        query_grad = (
            jnp.einsum("hbl,lhd->bhd", score_grad, key_rows, preferred_element_type=jnp.float32)
            * score_scale
        )
        key_grad = (
            key_grad
            + jnp.einsum(
                "hbl,bhd->lhd", score_grad, query_block, preferred_element_type=jnp.float32
            )
            * score_scale
        )
        return ((key_grad, value_grad), query_grad)

    firsts = jnp.arange(length_total // block_size, dtype=jnp.int32) * block_size
    zero_grad = jnp.zeros(key_rows.shape, jnp.float32)
    (key_grad, value_grad), query_grads = lax.scan(
        one_block, (zero_grad, zero_grad), (firsts, log_totals)
    )
    return (query_grads.reshape(key_rows.shape), key_grad, value_grad)


def reduce_rows(term_rows, row_share):
    return lax.psum_scatter(
        term_rows(jnp.int32(0), row_share * lax.axis_size("fsdp")).astype(jnp.bfloat16),
        "fsdp",
        scatter_dimension=0,
        tiled=True,
    ).astype(jnp.float32)


def per_device(
    tokens,
    teacher,
    segments,
    valid,
    ln1_gain,
    ln1_bias,
    w_qkv,
    b_qkv,
    w_out,
    ln2_gain,
    ln2_bias,
    w_gate_up,
    w_down,
):
    seq_count = lax.axis_size("seq")
    fsdp_count = lax.axis_size("fsdp")
    seq_index = lax.axis_index("seq")
    fsdp_index = lax.axis_index("fsdp")
    row_count = tokens.shape[1]
    model_width = tokens.shape[2]
    length_total = segments.shape[1]
    heads_here = H // seq_count
    group_width = heads_here * HD
    block_size = min(512, length_total)
    score_scale = HD ** (-0.5)
    tokens_total = row_count * seq_count * fsdp_count
    full_qkv, full_out, full_bias, gain_one, shift_one, gain_two, shift_two = (
        lax.all_gather(w_qkv, "fsdp", axis=0, tiled=True),
        lax.all_gather(w_out, "fsdp", axis=0, tiled=True),
        lax.all_gather(b_qkv, "fsdp", axis=0, tiled=True),
        lax.all_gather(ln1_gain, "fsdp", axis=0, tiled=True),
        lax.all_gather(ln1_bias, "fsdp", axis=0, tiled=True),
        lax.all_gather(ln2_gain, "fsdp", axis=0, tiled=True),
        lax.all_gather(ln2_bias, "fsdp", axis=0, tiled=True),
    )
    gain_one = gain_one.astype(jnp.float32)
    gain_two = gain_two.astype(jnp.float32)
    segment = segments[0]
    positions_all = doc_positions(segment)
    positions = lax.dynamic_slice_in_dim(positions_all, seq_index * row_count, row_count, 0)
    tokens_in = tokens[0].astype(jnp.float32)
    teacher_in = teacher[0].astype(jnp.float32)
    counted = valid[0].astype(jnp.float32)
    normed_one, inv_std_one = norm_parts(tokens_in)
    hidden_one = (normed_one * gain_one + shift_one.astype(jnp.float32)).astype(jnp.bfloat16)
    qkv_float = jnp.dot(
        hidden_one, full_qkv, preferred_element_type=jnp.float32
    ) + full_bias.astype(jnp.float32)
    split_rows = qkv_float.reshape(row_count, 3, H, HD)
    packed = jnp.stack(
        [
            rotate(split_rows[:, 0], positions, 1.0),
            rotate(split_rows[:, 1], positions, 1.0),
            split_rows[:, 2],
        ],
        axis=1,
    )
    packed = packed.astype(jnp.bfloat16).reshape(row_count, 3, seq_count, group_width)
    spread = lax.all_to_all(packed, "seq", split_axis=2, concat_axis=0, tiled=True)
    head_rows = spread.reshape(length_total, 3, heads_here, HD)
    query_rows = head_rows[:, 0]
    key_rows = head_rows[:, 1]
    value_rows = head_rows[:, 2]
    heads_out, log_totals = attention_forward(
        query_rows, key_rows, value_rows, segment, block_size, score_scale
    )
    returned = lax.all_to_all(
        heads_out.reshape(length_total, 1, group_width),
        "seq",
        split_axis=0,
        concat_axis=1,
        tiled=True,
    )
    attn_rows = returned.reshape(row_count, model_width)
    resid = tokens_in + jnp.dot(attn_rows, full_out, preferred_element_type=jnp.float32)
    normed_two, inv_std_two = norm_parts(resid)
    hidden_two = (normed_two * gain_two + shift_two.astype(jnp.float32)).astype(jnp.bfloat16)
    piece_gate = lax.all_gather(w_gate_up, "fsdp", axis=0, tiled=True)
    piece_down = lax.all_gather(w_down, "fsdp", axis=0, tiled=True)
    gate_up = jnp.einsum("td,ukd->tku", hidden_two, piece_gate, preferred_element_type=jnp.float32)
    hidden_piece = (jax.nn.silu(gate_up[:, 0]) * gate_up[:, 1]).astype(jnp.bfloat16)
    running = jnp.dot(hidden_piece, piece_down, preferred_element_type=jnp.float32)
    outputs = resid + running
    differ = outputs - teacher_in
    cot = counted[:, None] * differ
    half_sum = 0.5 * jnp.sum(cot * differ)
    count_here = jnp.sum(counted)
    cot_low = cot.astype(jnp.bfloat16)
    piece_gate = lax.all_gather(w_gate_up, "fsdp", axis=0, tiled=True)
    piece_down = lax.all_gather(w_down, "fsdp", axis=0, tiled=True)
    hidden_grad = jnp.einsum("tc,uc->tu", cot_low, piece_down, preferred_element_type=jnp.float32)
    piece_grads = gate_backward(gate_up, hidden_grad)
    grad_running = jnp.einsum(
        "tku,ukd->td", piece_grads, piece_gate, preferred_element_type=jnp.float32
    )

    def unit_rows(first_row, row_total):
        gate_term = jnp.einsum(
            "tku,td->ukd", piece_grads, hidden_two, preferred_element_type=jnp.float32
        )
        down_term = jnp.einsum(
            "tu,td->ud", hidden_piece, cot_low, preferred_element_type=jnp.float32
        )
        return jnp.concatenate([gate_term, down_term[:, None]], axis=1)

    ff_shard = reduce_rows(unit_rows, w_down.shape[0])
    resid_grad = cot + norm_back(grad_running, normed_two, inv_std_two, gain_two)
    gain_two_grad = jnp.sum(grad_running * normed_two, axis=0)
    shift_two_grad = jnp.sum(grad_running, axis=0)
    resid_low = resid_grad.astype(jnp.bfloat16)
    out_grad = jnp.einsum(
        "tc,ec->te", resid_low, full_out, preferred_element_type=jnp.float32
    ).astype(jnp.bfloat16)
    head_grad = lax.all_to_all(
        out_grad.reshape(row_count, seq_count, group_width),
        "seq",
        split_axis=1,
        concat_axis=0,
        tiled=True,
    )
    head_grad = head_grad.reshape(length_total, heads_here, HD)
    query_grad, key_grad, value_grad = attention_backward(
        query_rows, key_rows, value_rows, head_grad, log_totals, segment, block_size, score_scale
    )
    back_packed = jnp.stack(
        [
            rotate(query_grad, positions_all, -1.0),
            rotate(key_grad, positions_all, -1.0),
            value_grad,
        ],
        axis=1,
    )
    back_packed = back_packed.astype(jnp.bfloat16).reshape(length_total, 3, 1, group_width)
    qkv_grad = lax.all_to_all(back_packed, "seq", split_axis=0, concat_axis=2, tiled=True).reshape(
        row_count, 3 * model_width
    )
    grad_one = jnp.einsum("tc,ec->te", qkv_grad, full_qkv, preferred_element_type=jnp.float32)
    tokens_grad = resid_grad + norm_back(grad_one, normed_one, inv_std_one, gain_one)
    gain_one_grad = jnp.sum(grad_one * normed_one, axis=0)
    shift_one_grad = jnp.sum(grad_one, axis=0)
    bias_grad = jnp.sum(qkv_grad.astype(jnp.float32), axis=0)

    def feature_rows(first_row, row_total):
        qkv_term = jnp.einsum("tr,tc->rc", hidden_one, qkv_grad, preferred_element_type=jnp.float32)
        out_term = jnp.einsum("tr,tc->rc", attn_rows, resid_low, preferred_element_type=jnp.float32)
        return jnp.concatenate([qkv_term, out_term], axis=1)

    attn_shard = reduce_rows(feature_rows, w_qkv.shape[0])
    attn_total, ff_total = (
        lax.psum(attn_shard.astype(jnp.bfloat16), "seq").astype(jnp.float32),
        lax.psum(ff_shard.astype(jnp.bfloat16), "seq").astype(jnp.float32),
    )
    (
        sum_half,
        sum_count,
        total_gain_one,
        total_shift_one,
        total_gain_two,
        total_shift_two,
        total_bias,
    ) = lax.psum(
        (
            half_sum,
            count_here,
            gain_one_grad,
            shift_one_grad,
            gain_two_grad,
            shift_two_grad,
            bias_grad,
        ),
        ("seq", "fsdp"),
    )
    factor = tokens_total / sum_count
    loss = 2.0 * sum_half / (sum_count * model_width)

    def own_part(total_vec):
        share = total_vec.shape[0] // fsdp_count
        return factor * lax.dynamic_slice_in_dim(total_vec, fsdp_index * share, share, 0)

    layer_out = outputs.astype(jnp.bfloat16)[None]
    grad_tokens = (factor * tokens_grad).astype(jnp.bfloat16)[None]
    return (
        layer_out,
        loss,
        grad_tokens,
        own_part(total_gain_one),
        own_part(total_shift_one),
        factor * attn_total[:, : 3 * model_width],
        own_part(total_bias),
        factor * attn_total[:, 3 * model_width :],
        own_part(total_gain_two),
        own_part(total_shift_two),
        factor * ff_total[:, :2],
        factor * ff_total[:, 2],
    )


def solution(mesh):
    placed = (
        P("fsdp", "seq", None),
        P("fsdp", "seq", None),
        P("fsdp", None),
        P("fsdp", "seq"),
        P("fsdp"),
        P("fsdp"),
        P("fsdp", None),
        P("fsdp"),
        P("fsdp", None),
        P("fsdp"),
        P("fsdp"),
        P("fsdp", None, None),
        P("fsdp", None),
    )
    return jax.shard_map(
        per_device,
        mesh=mesh,
        in_specs=placed,
        out_specs=(
            P("fsdp", "seq", None),
            P(),
            P("fsdp", "seq", None),
            P("fsdp"),
            P("fsdp"),
            P("fsdp", None),
            P("fsdp"),
            P("fsdp", None),
            P("fsdp"),
            P("fsdp"),
            P("fsdp", None, None),
            P("fsdp", None),
        ),
        check_vma=False,
    )
```

profile of v0, /device:TPU:0, one launch (start us, length us, event | category | flops | bytes accessed | tf_op | source)
XLA Modules:
  0.0 4082.9 jit_solution(5188963605835579992)
XLA Ops:
  8.7 7.8 copy.122
  17.8 48.8 %all-gather.1 = bf16[8,1,256]{2,1,0:T(2,128)(2,1)S(1)} all-gather(bf16[1,1,256]{2,1,0:T(2,128)(2,1)S(1)} %reshape.465), channel_id=1, replica_groups=mesh['seq'=4,'fsdp'=8] {'fsdp'}, dimensions={0}, use_global_device_ids=true | all-gather | bytes 4608 | tf_op jit(solution)/shard_map/all_gather | solution.py:180
  66.6 30.9 all-gather
  97.5 39.9 all-gather.2
  139.2 354.2 %all-gather.10.cloned.1.call-done = bf16[2048,6144]{1,0:T(8,128)(2,1)} async-done(((bf16[256,6144]{1,0:T(8,128)(2,1)}), bf16[2048,6144]{1,0:T(8,128)(2,1)}) %all-gather.10.cloned.1.call-update) | async-done | bytes 25165840 | tf_op jit(solution)/shard_map/all_gather | solution.py:176
  493.4 13.4 convolution_add_fusion
  506.8 6.6 copy.116
  524.5 36.8 all-to-all-done
  565.4 6.1 reshape.456
  575.3 37.4 while.27
  579.2 4.7 fusion.125
  583.9 4.2 fusion.126
  588.1 5.9 fusion.127
  597.9 4.7 fusion.125
  602.6 4.2 fusion.126
  606.8 5.9 fusion.127
  615.3 7.2 reshape.481
  623.0 8.1 reduce.8
  638.5 64.3 %all-gather.4 = bf16[8,1,256]{2,1,0:T(2,128)(2,1)S(1)} all-gather(bf16[1,1,256]{2,1,0:T(2,128)(2,1)S(1)} %reshape.471), channel_id=1, replica_groups=mesh['seq'=4,'fsdp'=8] {'fsdp'}, dimensions={0}, use_global_device_ids=true | all-gather | bytes 4608 | tf_op jit(solution)/shard_map/all_gather | solution.py:182
  702.8 30.6 all-gather.3
  739.2 6.3 fusion.77
  745.9 748.3 %all-gather.14.cloned.1.call-done = bf16[5632,2,2048]{2,0,1:T(8,128)(2,1)} async-done(((bf16[704,2,2048]{2,0,1:T(8,128)(2,1)}), bf16[5632,2,2048]{2,0,1:T(8,128)(2,1)}) %all-gather.14.cloned.1.call-update) | async-done | bytes 46137360 | tf_op jit(solution)/shard_map/all_gather | solution.py:226
  1494.3 23.7 convolution_bitcast_fusion
  1518.0 6.3 multiply_convert_fusion.2
  1524.3 412.4 %all-gather.16.cloned.1.call-done = bf16[5632,2048]{1,0:T(8,128)(2,1)} async-done(((bf16[704,2048]{1,0:T(8,128)(2,1)}), bf16[5632,2048]{1,0:T(8,128)(2,1)}) %all-gather.16.cloned.1.call-update) | async-done | bytes 23068688 | tf_op jit(solution)/shard_map/all_gather | solution.py:227
  1936.7 12.5 multiply_convert_fusion.3
  1949.2 12.6 convert_bitcast_fusion.1
  1961.9 25.6 fusion.31
  1987.4 21.2 convert_bitcast_fusion
  2008.6 46.8 %pad_maximum_fusion = bf16[5632,3,2048]{0,2,1:T(8,128)(2,1)} fusion(bf16[5632,1,2048]{0,2,1:T(8,128)(2,1)} %convert_bitcast_fusion.1, bf16[5632,2,2048]{0,2,1:T(8,128)(2,1)} %convert_bitcast_fusion), kind=kLoop, calls=%fused_computation.40 | loop fusion | flops 34603008 | bytes 138412032 | tf_op jit(solution)/shard_map/concatenate | solution.py:252
  2055.4 88.8 %copy.142 = bf16[5632,6144]{1,0:T(8,128)(2,1)} copy(bf16[5632,6144]{0,1:T(8,128)(2,1)} %bitcast.64) | data formatting | bytes 138412032
  2144.3 22.0 multiply_reduce_fusion.1
  2169.4 6.5 convolution_convert_fusion.2
  2181.6 13.5 all-to-all-done.2
  2197.4 154.1 %while.28 = (s32[]{:T(128)}, f32[1024,8,64]{0,2,1:T(8,128)}, f32[1024,8,64]{0,2,1:T(8,128)}, f32[2,512,8,64]{1,0,3,2:T(2,128)}, s32[2]{0:T(128)S(1)}, /*index=5*...) while((s32[]{:T(128)}, f32[1024,8,64]{0,2,1:T(8,128)}, ...), condition=%wide.region_18.19_spmd.clone, body=%wide.region_16.18_spmd.clone.sunk | while | flops 2726556160 | bytes 233929072 | solution.py:133
  2201.5 9.8 fusion.137
  2211.3 13.8 multiply_reduce_fusion.7
  2225.1 11.9 multiply_convert_fusion.5
  2254.5 19.7 dynamic_update_slice.20
  2278.0 9.8 fusion.137
  2287.8 13.9 multiply_reduce_fusion.7
  2301.7 11.7 multiply_convert_fusion.5
  2317.5 4.7 bitcast_add_fusion.5
  2331.7 19.6 dynamic_update_slice.20
  2351.5 4.2 reshape.460
  2359.9 5.7 copy.126
  2365.6 5.1 all-to-all-start.3
  2370.8 5.7 convolution_convert_fusion.1
  2376.5 42.4 %all-to-all-done.3 = bf16[1024,3,1,512]{3,1,2,0:T(4,128)(2,1)} async-done(((bf16[1024,3,1,512]{3,1,2,0:T(4,128)(2,1)}), bf16[1024,3,1,512]{3,1,2,0:T(4,128)(2,1)}, u32[]{:S(2)}, u32[]{:S(2)}) %all-to-all-start.3) | async-done | bytes 3145760 | tf_op jit(solution)/shard_map/all_to_all | solution.py:282
  2418.9 4.7 copy.127
  2423.7 4.8 copy.128
  2428.5 14.3 convolution_convert_fusion
  2442.9 22.9 pad_maximum_fusion.1
  2465.8 764.0 %reduce-scatter.7.cloned.1.call-done = bf16[704,6144]{1,0:T(8,128)(2,1)} async-done(((bf16[5632,6144]{1,0:T(8,128)(2,1)}), bf16[704,6144]{1,0:T(8,128)(2,1)}) %reduce-scatter.7.cloned.1.call-update) | async-done | bytes 8650768
  3229.8 12.8 copy.143
  3242.6 529.5 %reduce-scatter.5.cloned.1.call-done = bf16[256,8192]{1,0:T(8,128)(2,1)} async-done(((bf16[2048,8192]{1,0:T(8,128)(2,1)}), bf16[256,8192]{1,0:T(8,128)(2,1)}) %reduce-scatter.5.cloned.1.call-update) | async-done | bytes 4194320 | tf_op jit(solution)/shard_map/reduce_scatter | solution.py:140
  3776.4 15.2 fusion.49
  3791.6 41.5 %all-reduce = (f32[]{:T(128)}, f32[]{:T(128)}, f32[2048]{0:T(1024)S(1)}, f32[2048]{0:T(1024)S(1)}, f32[6144]{0:T(1024)S(1)}, /*index=5*/f32[2048]{0:T(1024)S(1)}, f32[2048]{0:T(1024)S(1)}) all-reduce(f32[]{:T(128)S(6)} %mul_shard_map.3, f32[]{:T(128)} %convert_reduce_fusion.2, ...), channel_id=1, replica_groups=mesh['seq'=4,'fsdp'=8] {'seq','fsdp'}, use_global_device_ids=true, to_apply=%region_11.12 | all-reduce | flops 14338 | bytes 114704 | tf_op jit(solution)/shard_map/psum | solution.py:309
  3841.8 171.7 %all-reduce.4.cloned.1.call-done = (bf16[256,8192]{1,0:T(8,128)(2,1)}, bf16[704,3,2048]{0,2,1:T(8,128)(2,1)}) async-done(((bf16[256,8192]{1,0:T(8,128)(2,1)}, bf16[704,3,2048]{0,2,1:T(8,128)(2,1)}), (bf16[256,8192]{1,0:T(8,128)(2,1)}, bf16[704,3,2048]{0,2,1:T(8,128)(2,1)})) %all-reduce.4.cloned.1.call-update) | async-done | bytes 12845072 | tf_op jit(solution)/shard_map/psum | solution.py:298
  4021.3 11.8 convert_element_type.146
  4033.1 5.9 fusion.27
  4039.0 10.0 slice_multiply_fusion
  4049.0 19.1 copy.132
  4068.1 6.4 copy.133
  (228 shorter events, 111.9 us)
Async XLA Ops:
  7.2 486.2 %all-gather.10.cloned.1.call-start = ((), (), s32[]{:S(2)}) async-start(), calls=%async_computation.6 | async-start | bytes 28311552 | tf_op jit(solution)/shard_map/all_gather | solution.py:176
  7.9 731.3 %all-gather.12.cloned.1.call-start = ((), (), s32[]{:S(2)}) async-start(), calls=%async_computation.7 | async-start | bytes 9437184 | tf_op jit(solution)/shard_map/all_gather | solution.py:177
  8.7 1485.6 %all-gather.14.cloned.1.call-start = ((), (), s32[]{:S(2)}) async-start(), calls=%async_computation.8 | async-start | bytes 51904512 | tf_op jit(solution)/shard_map/all_gather | solution.py:226
  16.5 0.7 copy-start.42
  16.5 0.7 copy-start.43
  16.5 0.7 copy-start.39
  16.5 0.7 copy-start.15
  16.5 121.9 %copy-start.8 = (bf16[1,256,2048]{2,1,0:T(8,128)(2,1)S(1)}, bf16[1,256,2048]{2,1,0:T(8,128)(2,1)}, u32[]{:S(2)}) copy-start(bf16[1,256,2048]{2,1,0:T(8,128)(2,1)} %param.17) | copy-start | bytes 3145732
  16.6 1920.1 %all-gather.16.cloned.1.call-start = ((), (), s32[]{:S(2)}) async-start(), calls=%async_computation.9 | async-start | bytes 25952256 | tf_op jit(solution)/shard_map/all_gather | solution.py:227
  66.6 440.2 %copy-start.22 = (f32[8,1,256]{2,1,0:T(1,128)}, f32[8,1,256]{2,1,0:T(1,128)S(1)}, u32[]{:S(2)}) copy-start(f32[8,1,256]{2,1,0:T(1,128)S(1)} %convert_element_type.149) | copy-start | bytes 24580
  97.5 409.3 %copy-start.20 = (f32[8,1,256]{2,1,0:T(1,128)}, f32[8,1,256]{2,1,0:T(1,128)S(1)}, u32[]{:S(2)}) copy-start(f32[8,1,256]{2,1,0:T(1,128)S(1)} %convert_element_type.148) | copy-start | bytes 24580
  137.5 369.3 %copy-start.37 = (f32[8]{0:T(128)}, f32[8]{0:T(128)S(1)}, u32[]{:S(2)}) copy-start(f32[8]{0:T(128)S(1)} %multiply_power_fusion) | copy-start | bytes 100
  138.6 368.2 %copy-start.28 = (f32[256]{0:T(256)}, f32[256]{0:T(256)S(1)}, u32[]{:S(2)}) copy-start(f32[256]{0:T(256)S(1)} %broadcast_multiply_fusion.5) | copy-start | bytes 3076
  139.0 367.8 %copy-start.30 = (f32[256]{0:T(256)}, f32[256]{0:T(256)S(1)}, u32[]{:S(2)}) copy-start(f32[256]{0:T(256)S(1)} %add_rsqrt_fusion.1) | copy-start | bytes 3076
  520.6 40.8 all-to-all-start
  571.5 3.8 copy-start.19
  612.8 9.7 copy-start.24
  612.8 9.7 copy-start.46
  612.8 125.1 %copy-start.1 = (bf16[1024,8,64]{0,2,1:T(8,128)(2,1)}, bf16[1024,8,64]{0,2,1:T(8,128)(2,1)S(1)}, u32[]{:S(2)}) copy-start(bf16[1024,8,64]{0,2,1:T(8,128)(2,1)S(1)} %get-tuple-element.590) | copy-start | bytes 3145732
  623.0 15.4 copy-start.44
  623.0 15.4 copy-start.45
  623.0 15.5 copy-start.40
  634.8 98.6 %all-to-all-start.1 = ((bf16[4,2,65536]{2,1,0:T(2,128)(2,1)}), bf16[4,2,65536]{2,1,0:T(2,128)(2,1)S(1)}, u32[]{:S(2)}, u32[]{:S(2)}) async-start(bf16[4,2,65536]{2,1,0:T(2,128)(2,1)} %reshape.486), calls=%async_computation.1 | async-start | bytes 2097152 | tf_op jit(solution)/shard_map/all_to_all | solution.py:215
  638.4 2591.4 %reduce-scatter.7.cloned.1.call-start = ((), (), s32[]{:S(2)}) async-start(), calls=%async_computation.11 | async-start | bytes 77856768
  638.5 1298.2 %copy-start.35 = (f32[1,256]{1,0:T(1,128)}, f32[1,256]{1,0:T(1,128)S(1)}, u32[]{:S(2)}) copy-start(f32[1,256]{1,0:T(1,128)S(1)} %convert_element_type.133) | copy-start | bytes 3076
  735.9 3.3 copy-start.9
  1518.0 418.7 %copy-start.17 = (bf16[1,256,2048]{2,1,0:T(8,128)(2,1)S(1)}, bf16[1,256,2048]{2,1,0:T(8,128)(2,1)}, u32[]{:S(2)}) copy-start(bf16[1,256,2048]{2,1,0:T(8,128)(2,1)} %param.18) | copy-start | bytes 3145732
  2144.2 22.0 copy-start.14
  2144.2 22.0 copy-start.18
  2144.3 22.0 copy-start.36
  2169.4 6.6 copy-start.11
  2176.0 4.8 copy-start.32
  2176.0 4.8 copy-start.38
  2177.1 20.3 copy-start.2
  2177.1 20.3 copy-start.16
  2177.1 20.3 copy-start.25
  2177.1 20.3 copy-start.47
  2177.1 18.1 all-to-all-start.2
  2225.1 15.9 copy-start
  2245.0 4.1 copy-start.4
  2252.1 1.3 copy-start.5
  2253.4 20.7 copy-start.3
  2301.7 15.8 copy-start
  2322.3 4.0 copy-start.4
  2329.3 1.3 copy-start.5
  2330.6 20.7 copy-start.3
  2351.5 4.2 copy-start.6
  2355.7 2.2 copy-start.7
  2355.7 2.4 copy-start.26
  2355.7 2.4 copy-start.27
  2365.6 5.2 copy-start.12
  2365.6 5.2 copy-start.13
  2365.6 53.3 %all-to-all-start.3 = ((bf16[1024,3,1,512]{3,1,2,0:T(4,128)(2,1)}), bf16[1024,3,1,512]{3,1,2,0:T(4,128)(2,1)}, u32[]{:S(2)}, u32[]{:S(2)}) async-start(bf16[1024,3,1,512]{3,1,2,0:T(4,128)(2,1)} %copy.126), calls=%async_computation.3 | async-start | bytes 8388608 | tf_op jit(solution)/shard_map/all_to_all | solution.py:282
  2370.7 1401.4 %reduce-scatter.5.cloned.1.call-start = ((), (), s32[]{:S(2)}) async-start(), calls=%async_computation.10 | async-start | bytes 37748736 | tf_op jit(solution)/shard_map/reduce_scatter | solution.py:140
  2423.7 4.8 copy-start.10
  2423.7 4.8 copy-start.21
  2423.7 4.8 copy-start.23
  2423.7 4.8 copy-start.29
  2423.7 4.8 copy-start.31
  2465.8 1547.7 %all-reduce.4.cloned.1.call-start = ((), (), s32[]{:S(2)}) async-start(), calls=%async_computation.12 | async-start | bytes 27262976 | tf_op jit(solution)/shard_map/psum | solution.py:298
  3772.1 0.7 copy-start.41
  3776.4 15.2 copy-start.33
  3776.4 15.2 copy-start.34
Sparse Core Ops, SparseCore 0:
  9.5 483.8 all-gather.9
  495.5 124.4 all-gather.11
  622.1 872.0 all-gather.13
  1495.6 441.0 all-gather.15
  2144.4 1085.4 reduce-scatter.6
  3233.5 538.6 reduce-scatter.4
  3775.3 238.1 all-reduce.3
where the time goes:
time: 4100 us; the launch traced here: 4080 us
  waiting for transfers between devices  3070 us (75%)
  matrix products  270 us (7%)
  local copies, waits for them, and re-layouts  262 us (6%)
  blocking collectives  256 us (6%)
  other arithmetic  175 us (4%)
    unnamed x8, waiting for transfers between devices  766 us
    all_gather x1, waiting for transfers between devices, per_device(): piece_gate = lax.all_gather(w_gate_up, 'fsdp', axis=0, tiled=True)  748 us
    reduce_scatter x1, waiting for transfers between devices, reduce_rows(): lax.psum_scatter(term_rows(jnp.int32(0), row_share * lax.axis_size('fsdp'...  530 us
    all_gather x1, waiting for transfers between devices, per_device(): piece_down = lax.all_gather(w_down, 'fsdp', axis=0, tiled=True)  412 us
    all_gather x1, waiting for transfers between devices, per_device(): lax.all_gather(w_qkv, 'fsdp', axis=0, tiled=True)  354 us
    psum x1, waiting for transfers between devices, per_device(): lax.psum(attn_shard.astype(jnp.bfloat16), 'seq').astype(jnp.float32)  172 us
    unnamed x102, local copies, waits for them, and re-layouts  144 us
  transfers between devices with their start and end apart: 11, of which 9 were waited for; matrix products, arithmetic and copies ran while one was open for 10% of the time, Pallas kernels for 0%

commit v1 on v0

--- a/solution.py
+++ b/solution.py
@@ -8,6 +8,7 @@
 ROT = 16
 EPSILON = 1e-05
 MASKED_VALUE = -1e30
+notes_write = lambda mat, link_axis: lax.all_gather(mat, axis_name=link_axis).sum(axis=0)
 
 
 def norm_parts(values):
@@ -295,7 +296,7 @@
 
     attn_shard = reduce_rows(feature_rows, w_qkv.shape[0])
     attn_total, ff_total = (
-        lax.psum(attn_shard.astype(jnp.bfloat16), "seq").astype(jnp.float32),
+        notes_write(attn_shard.astype(jnp.bfloat16), link_axis="seq").astype(jnp.float32),
         lax.psum(ff_shard.astype(jnp.bfloat16), "seq").astype(jnp.float32),
     )
     (

time: 4100 us -> 4270 us (1.041)
  waiting for transfers between devices: 3070 us -> 3240 us
    unnamed x8 -> x9, waiting for transfers between devices: 766 us -> 1090 us
    reduce_scatter x1, waiting for transfers between devices: 530 us -> 367 us  [reduce_rows(): lax.psum_scatter(term_rows(jnp.int32(0), row_share * lax.axis_size('fsdp'...]
    unnamed x102 -> x112, local copies, waits for them, and re-layouts: 144 us -> 146 us
  transfers between devices with their start and end apart: 11 -> 12, of which waited for: 9 -> 10; matrix products, arithmetic and copies ran while one was open for 10% -> 9% of each run, Pallas kernels for 0% -> 0%
where the time goes in v1:
time: 4270 us; the launch traced here: 4250 us
  waiting for transfers between devices  3240 us (76%)
  local copies, waits for them, and re-layouts  264 us (6%)
  matrix products  259 us (6%)
  blocking collectives  256 us (6%)
  other arithmetic  189 us (4%)
    unnamed x9, waiting for transfers between devices  1090 us
    all_gather x1, waiting for transfers between devices, per_device(): piece_gate = lax.all_gather(w_gate_up, 'fsdp', axis=0, tiled=True)  747 us
    all_gather x1, waiting for transfers between devices, per_device(): piece_down = lax.all_gather(w_down, 'fsdp', axis=0, tiled=True)  412 us
    reduce_scatter x1, waiting for transfers between devices, reduce_rows(): lax.psum_scatter(term_rows(jnp.int32(0), row_share * lax.axis_size('fsdp'...  367 us
    all_gather x1, waiting for transfers between devices, per_device(): lax.all_gather(w_qkv, 'fsdp', axis=0, tiled=True)  354 us
    psum x1, waiting for transfers between devices, per_device(): lax.psum(ff_shard.astype(jnp.bfloat16), 'seq').astype(jnp.float32)  153 us
    unnamed x112, local copies, waits for them, and re-layouts  146 us
  transfers between devices with their start and end apart: 12, of which 10 were waited for; matrix products, arithmetic and copies ran while one was open for 9% of the time, Pallas kernels for 0%

profile of v1, /device:TPU:0, one launch (start us, length us, event | category | flops | bytes accessed | tf_op | source)
XLA Modules:
  0.0 4251.9 jit_solution(8990087259115370802)
XLA Ops:
  8.7 7.8 copy.122
  17.8 48.8 %all-gather.2 = bf16[8,1,256]{2,1,0:T(2,128)(2,1)S(1)} all-gather(bf16[1,1,256]{2,1,0:T(2,128)(2,1)S(1)} %reshape.466), channel_id=1, replica_groups=mesh['seq'=4,'fsdp'=8] {'fsdp'}, dimensions={0}, use_global_device_ids=true | all-gather | bytes 4608 | tf_op jit(solution)/shard_map/all_gather | solution.py:181
  66.6 30.9 all-gather.1
  97.5 39.9 all-gather.3
  139.2 354.2 %all-gather.12.cloned.1.call-done = bf16[2048,6144]{1,0:T(8,128)(2,1)} async-done(((bf16[256,6144]{1,0:T(8,128)(2,1)}), bf16[2048,6144]{1,0:T(8,128)(2,1)}) %all-gather.12.cloned.1.call-update) | async-done | bytes 25165840 | tf_op jit(solution)/shard_map/all_gather | solution.py:177
  493.4 13.4 convolution_add_fusion
  506.9 6.6 copy.116
  524.6 36.8 all-to-all-done
  565.5 6.1 reshape.456
  575.3 37.4 while.27
  579.2 4.7 fusion.125
  588.1 5.9 fusion.127
  597.9 4.7 fusion.125
  602.6 4.2 fusion.126
  606.8 5.9 fusion.127
  615.3 7.2 reshape.482
  622.9 8.1 reduce.9
  639.1 63.7 %all-gather.5 = bf16[8,1,256]{2,1,0:T(2,128)(2,1)S(1)} all-gather(bf16[1,1,256]{2,1,0:T(2,128)(2,1)S(1)} %reshape.472), channel_id=1, replica_groups=mesh['seq'=4,'fsdp'=8] {'fsdp'}, dimensions={0}, use_global_device_ids=true | all-gather | bytes 4608 | tf_op jit(solution)/shard_map/all_gather | solution.py:183
  702.8 30.6 all-gather.4
  739.8 6.5 fusion.77
  746.8 747.5 %all-gather.16.cloned.1.call-done = bf16[5632,2,2048]{2,0,1:T(8,128)(2,1)} async-done(((bf16[704,2,2048]{2,0,1:T(8,128)(2,1)}), bf16[5632,2,2048]{2,0,1:T(8,128)(2,1)}) %all-gather.16.cloned.1.call-update) | async-done | bytes 46137360 | tf_op jit(solution)/shard_map/all_gather | solution.py:227
  1494.3 23.7 convolution_bitcast_fusion
  1518.0 6.3 multiply_convert_fusion.2
  1524.3 412.4 %all-gather.18.cloned.1.call-done = bf16[5632,2048]{1,0:T(8,128)(2,1)} async-done(((bf16[704,2048]{1,0:T(8,128)(2,1)}), bf16[5632,2048]{1,0:T(8,128)(2,1)}) %all-gather.18.cloned.1.call-update) | async-done | bytes 23068688 | tf_op jit(solution)/shard_map/all_gather | solution.py:228
  1936.7 12.5 multiply_convert_fusion.3
  1949.2 17.7 fusion.31
  1966.9 21.7 multiply_reduce_fusion.1
  1988.6 4.4 multiply_add_fusion
  2000.9 13.5 all-to-all-done.2
  2016.7 152.0 %while.28 = (s32[]{:T(128)}, f32[1024,8,64]{0,2,1:T(8,128)}, f32[1024,8,64]{0,2,1:T(8,128)}, f32[2,512,8,64]{1,0,3,2:T(2,128)}, s32[2]{0:T(128)S(1)}, /*index=5*...) while((s32[]{:T(128)}, f32[1024,8,64]{0,2,1:T(8,128)}, ...), condition=%wide.region_18.19_spmd.clone, body=%wide.region_16.18_spmd.clone.sunk | while | flops 2726556160 | bytes 238123408 | solution.py:134
  2020.7 9.6 fusion.137
  2030.3 13.6 multiply_reduce_fusion.7
  2043.9 11.5 multiply_convert_fusion.5
  2072.8 19.6 dynamic_update_slice.20
  2096.3 9.6 fusion.137
  2105.9 13.6 multiply_reduce_fusion.7
  2119.5 11.5 multiply_convert_fusion.5
  2134.8 4.7 bitcast_add_fusion.5
  2149.0 19.6 dynamic_update_slice.20
  2176.9 5.7 copy.126
  2182.6 5.1 all-to-all-start.3
  2187.8 5.7 convolution_convert_fusion.1
  2193.5 42.4 all-to-all-done.3
  2235.9 4.6 copy.127
  2240.6 4.7 copy.128
  2245.3 13.9 convolution_convert_fusion
  2259.2 22.9 pad_maximum_fusion.1
  2283.4 12.8 convert_bitcast_fusion.1
  2296.2 21.3 convert_bitcast_fusion
  2317.5 47.1 %pad_maximum_fusion = bf16[5632,3,2048]{0,2,1:T(8,128)(2,1)} fusion(bf16[5632,1,2048]{0,2,1:T(8,128)(2,1)} %convert_bitcast_fusion.1, bf16[5632,2,2048]{0,2,1:T(8,128)(2,1)} %convert_bitcast_fusion), kind=kLoop, calls=%fused_computation.40 | loop fusion | flops 34603008 | bytes 138412032 | tf_op jit(solution)/shard_map/concatenate | solution.py:253
  2364.7 89.0 %copy.142 = bf16[5632,6144]{1,0:T(8,128)(2,1)} copy(bf16[5632,6144]{0,1:T(8,128)(2,1)} %bitcast.65) | data formatting | bytes 138412032
  2453.8 366.6 %reduce-scatter.5.cloned.1.call-done = bf16[256,8192]{1,0:T(8,128)(2,1)} async-done(((bf16[2048,8192]{1,0:T(8,128)(2,1)}), bf16[256,8192]{1,0:T(8,128)(2,1)}) %reduce-scatter.5.cloned.1.call-update) | async-done | bytes 4194320 | tf_op jit(solution)/shard_map/reduce_scatter | solution.py:141
  2821.7 1086.9 %reduce-scatter.7.cloned.1.call-done = bf16[704,6144]{1,0:T(8,128)(2,1)} async-done(((bf16[5632,6144]{1,0:T(8,128)(2,1)}), bf16[704,6144]{1,0:T(8,128)(2,1)}) %reduce-scatter.7.cloned.1.call-update) | async-done | bytes 8650768
  3908.6 12.5 copy.143
  3922.7 16.6 fusion.49
  3941.8 42.3 all-reduce
  3992.9 24.5 all-gather.20.cloned.1.call-done
  4017.4 12.3 reduce_sum.179
  4037.5 152.8 %all-reduce.3.cloned.1.call-done = bf16[704,3,2048]{0,2,1:T(8,128)(2,1)} async-done(((bf16[704,3,2048]{0,2,1:T(8,128)(2,1)}), bf16[704,3,2048]{0,2,1:T(8,128)(2,1)}) %all-reduce.3.cloned.1.call-update) | async-done | bytes 8650768 | tf_op jit(solution)/shard_map/psum | solution.py:300
  4190.3 11.8 convert_element_type.148
  4202.1 5.9 fusion.27
  4208.0 10.0 slice_multiply_fusion
  4218.0 19.1 copy.132
  4237.1 6.4 copy.133
  (247 shorter events, 122.5 us)
Async XLA Ops:
  7.2 486.2 %all-gather.12.cloned.1.call-start = ((), (), s32[]{:S(2)}) async-start(), calls=%async_computation.6 | async-start | bytes 28311552 | tf_op jit(solution)/shard_map/all_gather | solution.py:177
  7.9 731.9 %all-gather.14.cloned.1.call-start = ((), (), s32[]{:S(2)}) async-start(), calls=%async_computation.7 | async-start | bytes 9437184 | tf_op jit(solution)/shard_map/all_gather | solution.py:178
  8.7 1485.6 %all-gather.16.cloned.1.call-start = ((), (), s32[]{:S(2)}) async-start(), calls=%async_computation.8 | async-start | bytes 51904512 | tf_op jit(solution)/shard_map/all_gather | solution.py:227
  16.5 121.9 %copy-start.9 = (bf16[1,256,2048]{2,1,0:T(8,128)(2,1)S(1)}, bf16[1,256,2048]{2,1,0:T(8,128)(2,1)}, u32[]{:S(2)}) copy-start(bf16[1,256,2048]{2,1,0:T(8,128)(2,1)} %param.17) | copy-start | bytes 3145732
  16.6 1920.1 %all-gather.18.cloned.1.call-start = ((), (), s32[]{:S(2)}) async-start(), calls=%async_computation.9 | async-start | bytes 25952256 | tf_op jit(solution)/shard_map/all_gather | solution.py:228
  66.6 440.2 %copy-start.28 = (f32[8,1,256]{2,1,0:T(1,128)}, f32[8,1,256]{2,1,0:T(1,128)S(1)}, u32[]{:S(2)}) copy-start(f32[8,1,256]{2,1,0:T(1,128)S(1)} %convert_element_type.151) | copy-start | bytes 24580
  97.5 409.3 %copy-start.23 = (f32[8,1,256]{2,1,0:T(1,128)}, f32[8,1,256]{2,1,0:T(1,128)S(1)}, u32[]{:S(2)}) copy-start(f32[8,1,256]{2,1,0:T(1,128)S(1)} %convert_element_type.150) | copy-start | bytes 24580
  137.5 369.4 %copy-start.43 = (f32[8]{0:T(128)}, f32[8]{0:T(128)S(1)}, u32[]{:S(2)}) copy-start(f32[8]{0:T(128)S(1)} %multiply_power_fusion) | copy-start | bytes 100
  138.6 368.3 %copy-start.34 = (f32[256]{0:T(256)}, f32[256]{0:T(256)S(1)}, u32[]{:S(2)}) copy-start(f32[256]{0:T(256)S(1)} %broadcast_multiply_fusion.5) | copy-start | bytes 3076
  139.0 367.8 %copy-start.37 = (f32[256]{0:T(256)}, f32[256]{0:T(256)S(1)}, u32[]{:S(2)}) copy-start(f32[256]{0:T(256)S(1)} %add_rsqrt_fusion.1) | copy-start | bytes 3076
  520.6 40.8 all-to-all-start
  571.5 3.8 copy-start.21
  622.9 16.1 copy-start.50
  622.9 16.1 copy-start.51
  622.9 16.1 copy-start.46
  634.8 98.7 %all-to-all-start.1 = ((bf16[4,2,65536]{2,1,0:T(2,128)(2,1)}), bf16[4,2,65536]{2,1,0:T(2,128)(2,1)}, u32[]{:S(2)}, u32[]{:S(2)}) async-start(bf16[4,2,65536]{2,1,0:T(2,128)(2,1)} %reshape.487), calls=%async_computation.1 | async-start | bytes 2097152 | tf_op jit(solution)/shard_map/all_to_all | solution.py:216
  702.8 791.5 %copy-start.18 = (f32[8,1,256]{2,1,0:T(1,128)}, f32[8,1,256]{2,1,0:T(1,128)S(1)}, u32[]{:S(2)}) copy-start(f32[8,1,256]{2,1,0:T(1,128)S(1)} %convert_element_type.154) | copy-start | bytes 24580
  733.5 1255.1 %copy-start.16 = (f32[8,1,256]{2,1,0:T(1,128)}, f32[8,1,256]{2,1,0:T(1,128)S(1)}, u32[]{:S(2)}) copy-start(f32[8,1,256]{2,1,0:T(1,128)S(1)} %convert_element_type.153) | copy-start | bytes 24580
  746.4 1242.2 %copy-start.7 = (f32[256,2048]{1,0:T(8,128)}, f32[256,2048]{1,0:T(8,128)S(1)}, u32[]{:S(2)}) copy-start(f32[256,2048]{1,0:T(8,128)S(1)} %get-tuple-element.354) | copy-start | bytes 6291460
  746.4 1242.2 %copy-start.26 = (f32[256]{0:T(256)}, f32[256]{0:T(256)S(1)}, u32[]{:S(2)}) copy-start(f32[256]{0:T(256)S(1)} %broadcast_multiply_fusion.4) | copy-start | bytes 3076
  746.8 1241.8 %copy-start.30 = (f32[256]{0:T(256)}, f32[256]{0:T(256)S(1)}, u32[]{:S(2)}) copy-start(f32[256]{0:T(256)S(1)} %add_rsqrt_fusion) | copy-start | bytes 3076
  1949.2 43.8 %slice-start = ((s8[8388608]{0:T(1024)(128)(4,1)}), s8[4194304]{0:T(1024)(128)(4,1)S(1)}, s32[]{:S(2)}) async-start(s8[8388608]{0:T(1024)(128)(4,1)} %bitcast.249), calls=%async_computation.14 | async-start | bytes 8388608
  1966.9 26.1 slice-start.1
  1993.0 2.5 copy-start.12
  1995.5 4.6 copy-start.40
  1995.5 4.6 copy-start.44
  1996.6 17.9 all-to-all-start.2
  2016.7 13.6 copy-start.1
  2043.9 15.4 copy-start
  2063.3 4.0 copy-start.3
  2071.7 20.7 copy-start.2
  2092.4 13.5 copy-start.1
  2119.5 15.4 copy-start
  2139.6 4.0 copy-start.3
  2147.9 20.7 copy-start.2
  2168.7 4.2 copy-start.5
  2172.9 2.1 copy-start.6
  2172.9 2.2 copy-start.32
  2172.9 2.2 copy-start.33
  2182.6 5.2 copy-start.13
  2182.6 5.2 copy-start.15
  2182.6 53.3 %all-to-all-start.3 = ((bf16[1024,3,1,512]{3,1,2,0:T(4,128)(2,1)}), bf16[1024,3,1,512]{3,1,2,0:T(4,128)(2,1)}, u32[]{:S(2)}, u32[]{:S(2)}) async-start(bf16[1024,3,1,512]{3,1,2,0:T(4,128)(2,1)} %copy.126), calls=%async_computation.3 | async-start | bytes 8388608 | tf_op jit(solution)/shard_map/all_to_all | solution.py:283
  2187.7 632.7 %reduce-scatter.5.cloned.1.call-start = ((), (), s32[]{:S(2)}) async-start(), calls=%async_computation.10 | async-start | bytes 37748736 | tf_op jit(solution)/shard_map/reduce_scatter | solution.py:141
  2240.6 4.7 copy-start.10
  2240.6 4.7 copy-start.24
  2240.6 4.7 copy-start.29
  2240.6 4.8 copy-start.35
  2240.6 4.8 copy-start.38
  2282.2 14.0 copy-start.8
  2282.2 14.0 copy-start.17
  2282.2 14.0 copy-start.19
  2282.2 14.0 copy-start.27
  2282.2 14.0 copy-start.31
  2282.2 1626.4 %reduce-scatter.7.cloned.1.call-start = ((), (), s32[]{:S(2)}) async-start(), calls=%async_computation.13 | async-start | bytes 77856768
  2453.7 366.8 %copy-start.47 = (s32[1,256]{1,0:T(1,128)S(1)}, s32[1,256]{1,0:T(1,128)}, u32[]{:S(2)}) copy-start(s32[1,256]{1,0:T(1,128)} %param.20) | copy-start | bytes 3076
  2453.7 1563.7 %all-gather.20.cloned.1.call-start = ((), (), s32[]{:S(2)}) async-start(), calls=%async_computation.12 | async-start | bytes 20971520 | tf_op jit(solution)/shard_map/all_gather | solution.py:11
  2820.4 1369.8 %all-reduce.3.cloned.1.call-start = ((), (), s32[]{:S(2)}) async-start(), calls=%async_computation.11 | async-start | bytes 18874368 | tf_op jit(solution)/shard_map/psum | solution.py:300
  3921.1 1.6 copy-start.11
  3921.1 1.6 copy-start.25
  3921.1 1.6 copy-start.36
  3921.1 1.6 copy-start.39
  3939.3 2.5 copy-start.41
  3939.3 2.5 copy-start.42
  3939.3 50.1 %copy-start.14 = (f32[256,2048]{1,0:T(8,128)S(1)}, f32[256,2048]{1,0:T(8,128)}, u32[]{:S(2)}) copy-start(f32[256,2048]{1,0:T(8,128)} %copy-done.12) | copy-start | bytes 6291460
  (7 other events, 6.6 us)
Sparse Core Ops, SparseCore 0:
  9.5 483.8 all-gather.11
  495.5 124.4 all-gather.13
  622.1 872.0 all-gather.15
  1495.6 441.0 all-gather.17
  2282.3 538.0 reduce-scatter.4
  2824.2 1084.4 reduce-scatter.6
  3910.2 107.1 all-gather.19
  4020.4 169.7 all-reduce.2
